TPU v7x, 512 devices: a whole 4x8x8 slice. The times are simulated.
512 devices in a mesh: dp: 32 (over y, x), seq: 16 (over z, core).
Axes of the slice: x: 4, y: 8, z: 8, core: 2. Of those that a mesh axis runs over, the one named last changes fastest.
Arguments:
- states: bfloat16 [65536, 1280], P(('dp', 'seq')), parts along dimension 0, may hold values from -90 to 90
- token_kind: int32 [65536], P(('dp', 'seq')), parts along dimension 0, may hold values from 0 to 3
- episode: int32 [65536], P(('dp', 'seq')), parts along dimension 0, may hold values from 0 to 3, never falling along the last dimension, each value on 1 to 1536 neighbouring positions
- kind_table: bfloat16 [4, 1280], replicated, may hold values from -3 to 3
- w_qkv: bfloat16 [1280, 3072], replicated, may hold values from -0.15625 to 0.15625
- w_out: bfloat16 [1024, 1280], replicated, may hold values from -0.1875 to 0.1875
Outputs:
- attended: bfloat16 [65536, 1280], P(('dp', 'seq')), parts along dimension 0
There are 32 independent parts, one for each index of `dp`. A program takes and returns all parts, laid end to end along the dimension named above; an argument that names none is the same for every part. Nothing has to cross between parts.
All inputs are finite; a program needn't handle non-finite values.
Results may differ from a plain program's by a relative error of at most 0.0055.
The roundings to bfloat16 on the way count: a program that leaves them out, or rounds other values in their place, can miss the bound.
Values may be sent and summed in bfloat16 or wider, within the bound.
A program may use at most 128 MiB of HBM per device.

v0:
```python
import math
import jax
import jax.numpy as jnp
from jax import lax
from jax.sharding import PartitionSpec as P

HEADS = 16


def in_one_piece(arrays, axis, dim, along):
    both = jnp.concatenate(arrays, axis=along)
    result, at, gathered = (lax.all_gather(both, axis, axis=dim, tiled=True), 0, [])
    for a in arrays:
        gathered.append(lax.slice_in_dim(result, at, at + a.shape[along], axis=along))
        at += a.shape[along]
    return tuple(gathered)


def absorb(
    running, queries, query_place, query_episode, key_rows, value_rows, key_place, key_episode
):
    maxima, totals, summed = running
    temper = 1.0 / math.sqrt(queries.shape[2])
    scores = (
        jnp.einsum("qhd,khd->hqk", queries, key_rows, preferred_element_type=jnp.float32) * temper
    )
    allowed = (key_place[None, :] <= query_place[:, None]) & (
        key_episode[None, :] == query_episode[:, None]
    )
    scores = jnp.where(allowed[None], scores, -1e30)
    raised = jnp.maximum(maxima, jnp.max(scores, axis=2))
    shrink = jnp.exp(maxima - raised)
    weights = jnp.where(allowed[None], jnp.exp(scores - raised[:, :, None]), 0.0)
    totals = totals * shrink + jnp.sum(weights, axis=2)
    summed = summed * shrink.T[:, :, None] + jnp.einsum(
        "hqk,khd->qhd", weights.astype(jnp.bfloat16), value_rows, preferred_element_type=jnp.float32
    )
    return (raised, totals, summed)


def sweep_keys(
    running, queries, query_place, query_episode, key_rows, value_rows, key_place, key_episode
):
    length = key_rows.shape[0]
    stride = math.gcd(length, 512)

    def visit(number, current):
        offset = number * stride
        keys_here = lax.dynamic_slice_in_dim(key_rows, offset, stride, 0)
        values_here = lax.dynamic_slice_in_dim(value_rows, offset, stride, 0)
        place_here = lax.dynamic_slice_in_dim(key_place, offset, stride, 0)
        episode_here = lax.dynamic_slice_in_dim(key_episode, offset, stride, 0)
        skipped = (place_here[0] > query_place[-1]) | (episode_here[-1] < query_episode[0])
        return lax.cond(
            skipped,
            lambda s: s,
            lambda s: absorb(
                s,
                queries,
                query_place,
                query_episode,
                keys_here,
                values_here,
                place_here,
                episode_here,
            ),
            current,
        )

    return lax.fori_loop(0, length // stride, visit, running)


def fresh_state(count, heads, head_size):
    return (
        jnp.full((heads, count), -1e30, jnp.float32),
        jnp.zeros((heads, count), jnp.float32),
        jnp.zeros((count, heads, head_size), jnp.float32),
    )


def local(states, token_kind, episode, kind_table, w_qkv, w_out):
    rows = states.shape[0]
    kinds = kind_table.shape[0]
    picked = (token_kind[:, None] == jnp.arange(kinds, dtype=jnp.int32)[None, :]).astype(
        jnp.float32
    )
    added = jnp.dot(picked, kind_table.astype(jnp.float32))
    inputs = (states.astype(jnp.float32) + added).astype(jnp.bfloat16)
    projected = jnp.dot(inputs, w_qkv, preferred_element_type=jnp.float32).astype(jnp.bfloat16)
    inner = w_out.shape[0]
    head_size = inner // HEADS
    queries = projected[:, :inner].reshape(rows, HEADS, head_size)
    key_flat = projected[:, inner : 2 * inner]
    value_flat = projected[:, 2 * inner :]
    own_place = lax.axis_index("seq") * rows + jnp.arange(rows, dtype=jnp.int32)
    key_piece, value_piece, episode_piece = (
        *in_one_piece((key_flat, value_flat), "seq", 0, 1),
        lax.all_gather(episode, "seq", axis=0, tiled=True),
    )
    count = key_piece.shape[0]
    piece_place = jnp.arange(count, dtype=jnp.int32)
    maxima, totals, summed = sweep_keys(
        fresh_state(rows, HEADS, head_size),
        queries,
        own_place,
        episode,
        key_piece.reshape(count, HEADS, head_size),
        value_piece.reshape(count, HEADS, head_size),
        piece_place,
        episode_piece,
    )
    heads_out = (summed / totals.T[:, :, None]).astype(jnp.bfloat16).reshape(rows, inner)
    return jnp.dot(heads_out, w_out, preferred_element_type=jnp.float32).astype(jnp.bfloat16)


def solution(mesh):
    placed = (P(("dp", "seq"), None), P(("dp", "seq")), P(("dp", "seq")), P(), P(), P())
    return jax.shard_map(
        local, mesh=mesh, in_specs=placed, out_specs=P(("dp", "seq"), None), check_vma=False
    )
```

profile of v0, /device:TPU:387, one launch (start us, length us, event | category | flops | bytes accessed | tf_op | source)
XLA Modules:
  0.0 137.9 jit_solution(9066481034130938527)
XLA Ops:
  6.5 4.9 %convolution_convert_fusion = bf16[128,3072]{1,0:T(8,128)(2,1)S(1)} fusion(bf16[1280,3072]{1,0:T(8,128)(2,1)} %param.14, bf16[4,1280]{1,0:T(4,128)(2,1)} %param.13, bf16[128,1280]{1,0:T(8,128)(2,1)} %param.10, s32[128]{0:T(128)} %param.11), kind=kOutput, calls=%fused_computation.21 | convolution fusion | flops 1008828928 | bytes 8989184 | tf_op jit(solution)/shard_map/dot_general | solution.py:89
  13.1 1.1 copy.17
  14.2 14.9 %all-gather = s32[16,1,128]{2,1,0:T(1,128)S(1)} all-gather(s32[1,1,128]{2,1,0:T(1,128)S(1)} %bitcast.45), channel_id=1, replica_groups=mesh['dp'=32,'seq'=16] {'seq'}, dimensions={0}, use_global_device_ids=true | all-gather | bytes 8704 | tf_op jit(solution)/shard_map/all_gather | solution.py:98
  29.1 40.7 %all-gather.3.cloned.1.call-done = bf16[2048,2048]{1,0:T(8,128)(2,1)} async-done(((bf16[128,2048]{1,0:T(8,128)(2,1)}), bf16[2048,2048]{1,0:T(8,128)(2,1)}) %all-gather.3.cloned.1.call-update) | async-done | bytes 8388624 | tf_op jit(solution)/shard_map/all_gather | solution.py:12
  69.8 5.9 %fusion.25 = (bf16[2048,1024]{1,0:T(8,128)(2,1)}, bf16[2048,1024]{1,0:T(8,128)(2,1)}) fusion(bf16[2048,2048]{1,0:T(8,128)(2,1)} %all-gather.3.cloned.1.call-done), kind=kLoop, calls=%fused_computation.30 | loop fusion | bytes 16777216 | tf_op jit(solution)/shard_map/slice | solution.py:14
  75.7 6.5 %copy.16 = bf16[2048,1024]{0,1:T(8,128)(2,1)} copy(bf16[2048,1024]{1,0:T(8,128)(2,1)} %get-tuple-element.331) | data formatting | bytes 8388608 | tf_op jit(solution)/shard_map/slice | solution.py:14
  82.2 6.5 %copy.18 = bf16[2048,1024]{0,1:T(8,128)(2,1)} copy(bf16[2048,1024]{1,0:T(8,128)(2,1)} %get-tuple-element.330) | data formatting | bytes 8388608 | tf_op jit(solution)/shard_map/slice | solution.py:14
  88.8 40.9 %while.17 = (s32[]{:T(128)}, f32[16,128]{1,0:T(8,128)S(1)}, f32[16,128]{1,0:T(8,128)S(1)}, f32[128,16,64]{0,2,1:T(8,128)S(1)}, s32[2048]{0:T(1024)S(1)}, /*index...) while((s32[]{:T(128)}, f32[16,128]{1,0:T(8,128)S(1)}, ...), condition=%wide.region_5.6_spmd, body=%wide.region_0.5_spmd.sunk | while | flops 282531840 | bytes 16398717 | solution.py:70
  92.8 6.2 %conditional.2 = (f32[16,128]{1,0:T(8,128)S(1)}, f32[16,128]{1,0:T(8,128)S(1)}, f32[128,16,64]{0,2,1:T(8,128)S(1)}) conditional(s32[]{:T(128)} %bitcast.38, (s32[512]{0:T(512)S(1)}, s32[128]{0:T(128)S(1)}, s32[512]{0:T(512)S(1)}, s32[128]{0:T(128)S(1)}, bf16[2048,16,64]{0,2,1:T(8,128)(2,1)}, /*index=5*/s32[]{:T(128)}, ...), branch_computations={%region_1.3_spmd, %region_4.4_spmd} | conditional | flops 282531840 | bytes 16373784 | solution.py:54
  93.0 2.2 %fusion = (f32[16,128]{1,0:T(8,128)S(1)}, f32[16,512,128]{2,1,0:T(8,128)S(1)}) fusion(pred[128,512]{0,1:T(8,128)(4,1)S(1)} %compare_and_fusion, bf16[128,16,64]{0,2,1:T(8,128)(2,1)S(1)} %get-tuple-element.270, bf16[2048,16,64]{0,2,1:T(8,128)(2,1)} %get-tuple-element.268, s32[]{:T(128)} %get-tuple-element.269), kind=kOutput, calls=%fused_computation.2 | convolution fusion | flops 137361408 | bytes 5579264 | tf_op jit(solution)/shard_map/while/body/eval_jaxpr/cond/branch_0_fun/qhd,khd->hqk/dot_general | solution.py:25
  95.3 2.7 %fusion.9 = f32[128,16,64]{0,2,1:T(8,128)S(1)} fusion(f32[16,512,128]{2,1,0:T(8,128)S(1)} %get-tuple-element.329, f32[16,128]{1,0:T(8,128)S(1)} %get-tuple-element.405, pred[128,512]{0,1:T(8,128)(4,1)S(1)} %compare_and_fusion, bf16[2048,16,64]{0,2,1:T(8,128)(2,1)} %get-tuple-element.273, s32[]{:T(128)} %get-tuple-element.269, ...), kind=kOutput, calls=%fused_computation.8 | convolution fusion | flops 139722752 | bytes 6373888 | tf_op jit(solution)/shard_map/while/body/eval_jaxpr/cond/branch_0_fun/hqk,khd->qhd/dot_general | solution.py:35
  98.0 1.0 fusion.2
  103.0 6.2 %conditional.2 = (f32[16,128]{1,0:T(8,128)S(1)}, f32[16,128]{1,0:T(8,128)S(1)}, f32[128,16,64]{0,2,1:T(8,128)S(1)}) conditional(s32[]{:T(128)} %bitcast.38, (s32[512]{0:T(512)S(1)}, s32[128]{0:T(128)S(1)}, s32[512]{0:T(512)S(1)}, s32[128]{0:T(128)S(1)}, bf16[2048,16,64]{0,2,1:T(8,128)(2,1)}, /*index=5*/s32[]{:T(128)}, ...), branch_computations={%region_1.3_spmd, %region_4.4_spmd} | conditional | flops 282531840 | bytes 16373784 | solution.py:54
  103.2 2.2 %fusion = (f32[16,128]{1,0:T(8,128)S(1)}, f32[16,512,128]{2,1,0:T(8,128)S(1)}) fusion(pred[128,512]{0,1:T(8,128)(4,1)S(1)} %compare_and_fusion, bf16[128,16,64]{0,2,1:T(8,128)(2,1)S(1)} %get-tuple-element.270, bf16[2048,16,64]{0,2,1:T(8,128)(2,1)} %get-tuple-element.268, s32[]{:T(128)} %get-tuple-element.269), kind=kOutput, calls=%fused_computation.2 | convolution fusion | flops 137361408 | bytes 5579264 | tf_op jit(solution)/shard_map/while/body/eval_jaxpr/cond/branch_0_fun/qhd,khd->hqk/dot_general | solution.py:25
  105.5 2.7 %fusion.9 = f32[128,16,64]{0,2,1:T(8,128)S(1)} fusion(f32[16,512,128]{2,1,0:T(8,128)S(1)} %get-tuple-element.329, f32[16,128]{1,0:T(8,128)S(1)} %get-tuple-element.405, pred[128,512]{0,1:T(8,128)(4,1)S(1)} %compare_and_fusion, bf16[2048,16,64]{0,2,1:T(8,128)(2,1)} %get-tuple-element.273, s32[]{:T(128)} %get-tuple-element.269, ...), kind=kOutput, calls=%fused_computation.8 | convolution fusion | flops 139722752 | bytes 6373888 | tf_op jit(solution)/shard_map/while/body/eval_jaxpr/cond/branch_0_fun/hqk,khd->qhd/dot_general | solution.py:35
  108.2 1.0 fusion.2
  113.2 6.2 %conditional.2 = (f32[16,128]{1,0:T(8,128)S(1)}, f32[16,128]{1,0:T(8,128)S(1)}, f32[128,16,64]{0,2,1:T(8,128)S(1)}) conditional(s32[]{:T(128)} %bitcast.38, (s32[512]{0:T(512)S(1)}, s32[128]{0:T(128)S(1)}, s32[512]{0:T(512)S(1)}, s32[128]{0:T(128)S(1)}, bf16[2048,16,64]{0,2,1:T(8,128)(2,1)}, /*index=5*/s32[]{:T(128)}, ...), branch_computations={%region_1.3_spmd, %region_4.4_spmd} | conditional | flops 282531840 | bytes 16373784 | solution.py:54
  113.4 2.2 %fusion = (f32[16,128]{1,0:T(8,128)S(1)}, f32[16,512,128]{2,1,0:T(8,128)S(1)}) fusion(pred[128,512]{0,1:T(8,128)(4,1)S(1)} %compare_and_fusion, bf16[128,16,64]{0,2,1:T(8,128)(2,1)S(1)} %get-tuple-element.270, bf16[2048,16,64]{0,2,1:T(8,128)(2,1)} %get-tuple-element.268, s32[]{:T(128)} %get-tuple-element.269), kind=kOutput, calls=%fused_computation.2 | convolution fusion | flops 137361408 | bytes 5579264 | tf_op jit(solution)/shard_map/while/body/eval_jaxpr/cond/branch_0_fun/qhd,khd->hqk/dot_general | solution.py:25
  115.7 2.7 %fusion.9 = f32[128,16,64]{0,2,1:T(8,128)S(1)} fusion(f32[16,512,128]{2,1,0:T(8,128)S(1)} %get-tuple-element.329, f32[16,128]{1,0:T(8,128)S(1)} %get-tuple-element.405, pred[128,512]{0,1:T(8,128)(4,1)S(1)} %compare_and_fusion, bf16[2048,16,64]{0,2,1:T(8,128)(2,1)} %get-tuple-element.273, s32[]{:T(128)} %get-tuple-element.269, ...), kind=kOutput, calls=%fused_computation.8 | convolution fusion | flops 139722752 | bytes 6373888 | tf_op jit(solution)/shard_map/while/body/eval_jaxpr/cond/branch_0_fun/hqk,khd->qhd/dot_general | solution.py:35
  118.4 1.0 fusion.2
  123.4 6.2 %conditional.2 = (f32[16,128]{1,0:T(8,128)S(1)}, f32[16,128]{1,0:T(8,128)S(1)}, f32[128,16,64]{0,2,1:T(8,128)S(1)}) conditional(s32[]{:T(128)} %bitcast.38, (s32[512]{0:T(512)S(1)}, s32[128]{0:T(128)S(1)}, s32[512]{0:T(512)S(1)}, s32[128]{0:T(128)S(1)}, bf16[2048,16,64]{0,2,1:T(8,128)(2,1)}, /*index=5*/s32[]{:T(128)}, ...), branch_computations={%region_1.3_spmd, %region_4.4_spmd} | conditional | flops 282531840 | bytes 16373784 | solution.py:54
  123.7 2.2 %fusion = (f32[16,128]{1,0:T(8,128)S(1)}, f32[16,512,128]{2,1,0:T(8,128)S(1)}) fusion(pred[128,512]{0,1:T(8,128)(4,1)S(1)} %compare_and_fusion, bf16[128,16,64]{0,2,1:T(8,128)(2,1)S(1)} %get-tuple-element.270, bf16[2048,16,64]{0,2,1:T(8,128)(2,1)} %get-tuple-element.268, s32[]{:T(128)} %get-tuple-element.269), kind=kOutput, calls=%fused_computation.2 | convolution fusion | flops 137361408 | bytes 5579264 | tf_op jit(solution)/shard_map/while/body/eval_jaxpr/cond/branch_0_fun/qhd,khd->hqk/dot_general | solution.py:25
  125.9 2.7 %fusion.9 = f32[128,16,64]{0,2,1:T(8,128)S(1)} fusion(f32[16,512,128]{2,1,0:T(8,128)S(1)} %get-tuple-element.329, f32[16,128]{1,0:T(8,128)S(1)} %get-tuple-element.405, pred[128,512]{0,1:T(8,128)(4,1)S(1)} %compare_and_fusion, bf16[2048,16,64]{0,2,1:T(8,128)(2,1)} %get-tuple-element.273, s32[]{:T(128)} %get-tuple-element.269, ...), kind=kOutput, calls=%fused_computation.8 | convolution fusion | flops 139722752 | bytes 6373888 | tf_op jit(solution)/shard_map/while/body/eval_jaxpr/cond/branch_0_fun/hqk,khd->qhd/dot_general | solution.py:35
  129.7 1.3 convolution_convert_fusion.1
  (51 shorter events, 11.6 us)
Async XLA Ops:
  6.5 123.2 %copy-start = (bf16[1024,1280]{1,0:T(8,128)(2,1)S(1)}, bf16[1024,1280]{1,0:T(8,128)(2,1)}, u32[]{:S(2)}) copy-start(bf16[1024,1280]{1,0:T(8,128)(2,1)} %param.15) | copy-start | bytes 7864324
  6.5 7.6 %copy-start.1 = (s32[128]{0:T(128)S(1)}, s32[128]{0:T(128)}, u32[]{:S(2)}) copy-start(s32[128]{0:T(128)} %param.12) | copy-start | bytes 1540
  6.5 63.2 %all-gather.3.cloned.1.call-start = ((), (), s32[]{:S(2)}) async-start(), calls=%async_computation | async-start | bytes 8912896 | tf_op jit(solution)/shard_map/all_gather | solution.py:12
Sparse Core Ops, SparseCore 0:
  12.5 57.2 all-gather.2
where the time goes:
time: 139 us; the launch traced here: 138 us
  waiting for transfers between devices  40.7 us (29%)
  local copies, waits for them, and re-layouts  29.7 us (21%)
  matrix products  25.8 us (19%)
  blocking collectives  14.9 us (11%)
  between operations  13.5 us (10%)
  loops' own time  8.33 us (6%)
  other arithmetic  4.96 us (4%)
    all_gather x1, waiting for transfers between devices, in_one_piece(): lax.all_gather(both, axis, axis=dim, tiled=True)  40.7 us
    slice x3, local copies, waits for them, and re-layouts, in_one_piece(): lax.slice_in_dim(result, at, at + a.shape[along], axis=along)  18.9 us
    all_gather x1, blocking collectives, local(): lax.all_gather(episode, 'seq', axis=0, tiled=True)  14.9 us
    dot_general x4, matrix products, absorb(): jnp.einsum('hqk,khd->qhd', weights.astype(jnp.bfloat16), value_rows, pref...  10.7 us
    dot_general x4, matrix products, absorb(): jnp.einsum('qhd,khd->hqk', queries, key_rows, preferred_element_type=jnp....  8.94 us
    another operation x1, loops' own time, sweep_keys(): return lax.fori_loop(0, length // stride, visit, running)  8.14 us
    dot_general x1, matrix products, local(): jnp.dot(inputs, w_qkv, preferred_element_type=jnp.float32)  4.89 us
    reduce_sum x4, other arithmetic, absorb(): totals = totals * shrink + jnp.sum(weights, axis=2)  4.01 us
  transfers between devices with their start and end apart: 1, of which 1 were waited for; matrix products, arithmetic and copies ran while one was open for 1% of the time, Pallas kernels for 0%

commit v1 on v0

--- a/solution.py
+++ b/solution.py
@@ -93,9 +93,17 @@
     key_flat = projected[:, inner : 2 * inner]
     value_flat = projected[:, 2 * inner :]
     own_place = lax.axis_index("seq") * rows + jnp.arange(rows, dtype=jnp.int32)
+
+    def order_map(point):
+        part_now = jnp.concatenate(
+            lax.all_to_all(jnp.stack([point for _ in range(lax.axis_size("seq"))]), "seq", 0, 0),
+            axis=0,
+        )
+        return part_now
+
     key_piece, value_piece, episode_piece = (
         *in_one_piece((key_flat, value_flat), "seq", 0, 1),
-        lax.all_gather(episode, "seq", axis=0, tiled=True),
+        order_map(episode),
     )
     count = key_piece.shape[0]
     piece_place = jnp.arange(count, dtype=jnp.int32)

time: 139 us -> 140 us (level)
  blocking collectives: 14.9 us -> 0 us
  waiting for transfers between devices: 40.7 us -> 50 us
  starting transfers between devices: 0.01 us -> 5.72 us
    all_gather x1 -> x0, blocking collectives: 14.9 us -> none  [local(): lax.all_gather(episode, 'seq', axis=0, tiled=True)]
    all_gather x1, waiting for transfers between devices: 40.7 us -> 49.9 us  [in_one_piece(): lax.all_gather(both, axis, axis=dim, tiled=True)]
    all_to_all x0 -> x1, starting transfers between devices: none -> 5.72 us  [order_map(): lax.all_to_all(jnp.stack([point for _ in range(lax.axis_size('seq'))]), '...]
  transfers between devices with their start and end apart: 1 -> 2, of which waited for: 1 -> 1; matrix products, arithmetic and copies ran while one was open for 1% -> 15% of each run, Pallas kernels for 0% -> 0%
where the time goes in v1:
time: 140 us
  waiting for transfers between devices  50 us (36%)
  local copies, waits for them, and re-layouts  30.5 us (22%)
  matrix products  26.8 us (19%)
  between operations  13.5 us (10%)
  loops' own time  8.19 us (6%)
  starting transfers between devices  5.72 us (4%)
  other arithmetic  4.96 us (4%)
    all_gather x1, waiting for transfers between devices, in_one_piece(): lax.all_gather(both, axis, axis=dim, tiled=True)  49.9 us
    slice x3, local copies, waits for them, and re-layouts, in_one_piece(): lax.slice_in_dim(result, at, at + a.shape[along], axis=along)  18.9 us
    dot_general x4, matrix products, absorb(): jnp.einsum('hqk,khd->qhd', weights.astype(jnp.bfloat16), value_rows, pref...  10.7 us
    dot_general x4, matrix products, absorb(): jnp.einsum('qhd,khd->hqk', queries, key_rows, preferred_element_type=jnp....  8.94 us
    another operation x1, loops' own time, sweep_keys(): return lax.fori_loop(0, length // stride, visit, running)  8 us
    dot_general x1, matrix products, local(): jnp.dot(inputs, w_qkv, preferred_element_type=jnp.float32)  5.84 us
    all_to_all x1, starting transfers between devices, order_map(): lax.all_to_all(jnp.stack([point for _ in range(lax.axis_size('seq'))]), '...  5.72 us
    reduce_sum x4, other arithmetic, absorb(): totals = totals * shrink + jnp.sum(weights, axis=2)  4.01 us
  transfers between devices with their start and end apart: 2, of which 1 were waited for; matrix products, arithmetic and copies ran while one was open for 15% of the time, Pallas kernels for 0%

profile of v1, /device:TPU:387, one launch (start us, length us, event | category | flops | bytes accessed | tf_op | source)
XLA Modules:
  0.0 139.6 jit_solution(15195682838775643419)
XLA Ops:
  6.5 5.8 %convolution_convert_fusion = bf16[128,3072]{1,0:T(8,128)(2,1)} fusion(bf16[1280,3072]{1,0:T(8,128)(2,1)} %param.14, bf16[4,1280]{1,0:T(4,128)(2,1)} %param.13, bf16[128,1280]{1,0:T(8,128)(2,1)} %param.10, s32[128]{0:T(128)} %param.11), kind=kOutput, calls=%fused_computation.21 | convolution fusion | flops 1008828928 | bytes 8989184 | tf_op jit(solution)/shard_map/dot_general | solution.py:89
  12.4 1.9 %concatenate.4 = bf16[128,2048]{1,0:T(8,128)(2,1)} slice(bf16[128,3072]{1,0:T(8,128)(2,1)} %convolution_convert_fusion), slice={[0:128], [1024:3072]} | slice | bytes 1048576 | tf_op jit(solution)/shard_map/concatenate | solution.py:11
  14.9 5.7 %all-to-all-start = ((s32[16,1,128]{2,1,0:T(1,128)}), s32[16,1,128]{2,1,0:T(1,128)S(1)}, u32[]{:S(2)}, u32[]{:S(2)}) async-start(s32[16,1,128]{2,1,0:T(1,128)} %stack.2), calls=%async_computation | async-start | bytes 16384 | tf_op jit(solution)/shard_map/all_to_all | solution.py:99
  21.8 49.9 %all-gather.2.cloned.1.call-done = bf16[2048,2048]{1,0:T(8,128)(2,1)} async-done(((bf16[128,2048]{1,0:T(8,128)(2,1)}), bf16[2048,2048]{1,0:T(8,128)(2,1)}) %all-gather.2.cloned.1.call-update) | async-done | bytes 8388624 | tf_op jit(solution)/shard_map/all_gather | solution.py:12
  71.7 5.9 %fusion.25 = (bf16[2048,1024]{1,0:T(8,128)(2,1)}, bf16[2048,1024]{1,0:T(8,128)(2,1)}) fusion(bf16[2048,2048]{1,0:T(8,128)(2,1)} %all-gather.2.cloned.1.call-done), kind=kLoop, calls=%fused_computation.30 | loop fusion | bytes 16777216 | tf_op jit(solution)/shard_map/slice | solution.py:14
  77.6 6.5 %copy.12 = bf16[2048,1024]{0,1:T(8,128)(2,1)} copy(bf16[2048,1024]{1,0:T(8,128)(2,1)} %get-tuple-element.331) | data formatting | bytes 8388608 | tf_op jit(solution)/shard_map/slice | solution.py:14
  84.2 6.5 %copy.14 = bf16[2048,1024]{0,1:T(8,128)(2,1)} copy(bf16[2048,1024]{1,0:T(8,128)(2,1)} %get-tuple-element.330) | data formatting | bytes 8388608 | tf_op jit(solution)/shard_map/slice | solution.py:14
  90.7 40.6 %while.17 = (s32[]{:T(128)}, f32[16,128]{1,0:T(8,128)S(1)}, f32[16,128]{1,0:T(8,128)S(1)}, f32[128,16,64]{0,2,1:T(8,128)S(1)}, s32[2048]{0:T(1024)S(1)}, /*index...) while((s32[]{:T(128)}, f32[16,128]{1,0:T(8,128)S(1)}, ...), condition=%wide.region_5.6_spmd, body=%wide.region_0.5_spmd.sunk | while | flops 282531840 | bytes 16398717 | solution.py:70
  94.7 6.2 %conditional.2 = (f32[16,128]{1,0:T(8,128)S(1)}, f32[16,128]{1,0:T(8,128)S(1)}, f32[128,16,64]{0,2,1:T(8,128)S(1)}) conditional(s32[]{:T(128)} %bitcast.37, (s32[512]{0:T(512)S(1)}, s32[128]{0:T(128)S(1)}, s32[512]{0:T(512)S(1)}, s32[128]{0:T(128)S(1)}, bf16[2048,16,64]{0,2,1:T(8,128)(2,1)}, /*index=5*/s32[]{:T(128)}, ...), branch_computations={%region_1.3_spmd, %region_4.4_spmd} | conditional | flops 282531840 | bytes 16373784 | solution.py:54
  94.9 2.2 %fusion = (f32[16,128]{1,0:T(8,128)S(1)}, f32[16,512,128]{2,1,0:T(8,128)S(1)}) fusion(pred[128,512]{0,1:T(8,128)(4,1)S(1)} %compare_and_fusion, bf16[128,16,64]{0,2,1:T(8,128)(2,1)S(1)} %get-tuple-element.270, bf16[2048,16,64]{0,2,1:T(8,128)(2,1)} %get-tuple-element.268, s32[]{:T(128)} %get-tuple-element.269), kind=kOutput, calls=%fused_computation.2 | convolution fusion | flops 137361408 | bytes 5579264 | tf_op jit(solution)/shard_map/while/body/eval_jaxpr/cond/branch_0_fun/qhd,khd->hqk/dot_general | solution.py:25
  97.2 2.7 %fusion.9 = f32[128,16,64]{0,2,1:T(8,128)S(1)} fusion(f32[16,512,128]{2,1,0:T(8,128)S(1)} %get-tuple-element.329, f32[16,128]{1,0:T(8,128)S(1)} %get-tuple-element.405, pred[128,512]{0,1:T(8,128)(4,1)S(1)} %compare_and_fusion, bf16[2048,16,64]{0,2,1:T(8,128)(2,1)} %get-tuple-element.273, s32[]{:T(128)} %get-tuple-element.269, ...), kind=kOutput, calls=%fused_computation.8 | convolution fusion | flops 139722752 | bytes 6373888 | tf_op jit(solution)/shard_map/while/body/eval_jaxpr/cond/branch_0_fun/hqk,khd->qhd/dot_general | solution.py:35
  99.8 1.0 fusion.2
  104.8 6.2 %conditional.2 = (f32[16,128]{1,0:T(8,128)S(1)}, f32[16,128]{1,0:T(8,128)S(1)}, f32[128,16,64]{0,2,1:T(8,128)S(1)}) conditional(s32[]{:T(128)} %bitcast.37, (s32[512]{0:T(512)S(1)}, s32[128]{0:T(128)S(1)}, s32[512]{0:T(512)S(1)}, s32[128]{0:T(128)S(1)}, bf16[2048,16,64]{0,2,1:T(8,128)(2,1)}, /*index=5*/s32[]{:T(128)}, ...), branch_computations={%region_1.3_spmd, %region_4.4_spmd} | conditional | flops 282531840 | bytes 16373784 | solution.py:54
  105.1 2.2 %fusion = (f32[16,128]{1,0:T(8,128)S(1)}, f32[16,512,128]{2,1,0:T(8,128)S(1)}) fusion(pred[128,512]{0,1:T(8,128)(4,1)S(1)} %compare_and_fusion, bf16[128,16,64]{0,2,1:T(8,128)(2,1)S(1)} %get-tuple-element.270, bf16[2048,16,64]{0,2,1:T(8,128)(2,1)} %get-tuple-element.268, s32[]{:T(128)} %get-tuple-element.269), kind=kOutput, calls=%fused_computation.2 | convolution fusion | flops 137361408 | bytes 5579264 | tf_op jit(solution)/shard_map/while/body/eval_jaxpr/cond/branch_0_fun/qhd,khd->hqk/dot_general | solution.py:25
  107.3 2.7 %fusion.9 = f32[128,16,64]{0,2,1:T(8,128)S(1)} fusion(f32[16,512,128]{2,1,0:T(8,128)S(1)} %get-tuple-element.329, f32[16,128]{1,0:T(8,128)S(1)} %get-tuple-element.405, pred[128,512]{0,1:T(8,128)(4,1)S(1)} %compare_and_fusion, bf16[2048,16,64]{0,2,1:T(8,128)(2,1)} %get-tuple-element.273, s32[]{:T(128)} %get-tuple-element.269, ...), kind=kOutput, calls=%fused_computation.8 | convolution fusion | flops 139722752 | bytes 6373888 | tf_op jit(solution)/shard_map/while/body/eval_jaxpr/cond/branch_0_fun/hqk,khd->qhd/dot_general | solution.py:35
  110.0 1.0 fusion.2
  115.0 6.2 %conditional.2 = (f32[16,128]{1,0:T(8,128)S(1)}, f32[16,128]{1,0:T(8,128)S(1)}, f32[128,16,64]{0,2,1:T(8,128)S(1)}) conditional(s32[]{:T(128)} %bitcast.37, (s32[512]{0:T(512)S(1)}, s32[128]{0:T(128)S(1)}, s32[512]{0:T(512)S(1)}, s32[128]{0:T(128)S(1)}, bf16[2048,16,64]{0,2,1:T(8,128)(2,1)}, /*index=5*/s32[]{:T(128)}, ...), branch_computations={%region_1.3_spmd, %region_4.4_spmd} | conditional | flops 282531840 | bytes 16373784 | solution.py:54
  115.2 2.2 %fusion = (f32[16,128]{1,0:T(8,128)S(1)}, f32[16,512,128]{2,1,0:T(8,128)S(1)}) fusion(pred[128,512]{0,1:T(8,128)(4,1)S(1)} %compare_and_fusion, bf16[128,16,64]{0,2,1:T(8,128)(2,1)S(1)} %get-tuple-element.270, bf16[2048,16,64]{0,2,1:T(8,128)(2,1)} %get-tuple-element.268, s32[]{:T(128)} %get-tuple-element.269), kind=kOutput, calls=%fused_computation.2 | convolution fusion | flops 137361408 | bytes 5579264 | tf_op jit(solution)/shard_map/while/body/eval_jaxpr/cond/branch_0_fun/qhd,khd->hqk/dot_general | solution.py:25
  117.5 2.7 %fusion.9 = f32[128,16,64]{0,2,1:T(8,128)S(1)} fusion(f32[16,512,128]{2,1,0:T(8,128)S(1)} %get-tuple-element.329, f32[16,128]{1,0:T(8,128)S(1)} %get-tuple-element.405, pred[128,512]{0,1:T(8,128)(4,1)S(1)} %compare_and_fusion, bf16[2048,16,64]{0,2,1:T(8,128)(2,1)} %get-tuple-element.273, s32[]{:T(128)} %get-tuple-element.269, ...), kind=kOutput, calls=%fused_computation.8 | convolution fusion | flops 139722752 | bytes 6373888 | tf_op jit(solution)/shard_map/while/body/eval_jaxpr/cond/branch_0_fun/hqk,khd->qhd/dot_general | solution.py:35
  120.2 1.0 fusion.2
  125.2 6.2 %conditional.2 = (f32[16,128]{1,0:T(8,128)S(1)}, f32[16,128]{1,0:T(8,128)S(1)}, f32[128,16,64]{0,2,1:T(8,128)S(1)}) conditional(s32[]{:T(128)} %bitcast.37, (s32[512]{0:T(512)S(1)}, s32[128]{0:T(128)S(1)}, s32[512]{0:T(512)S(1)}, s32[128]{0:T(128)S(1)}, bf16[2048,16,64]{0,2,1:T(8,128)(2,1)}, /*index=5*/s32[]{:T(128)}, ...), branch_computations={%region_1.3_spmd, %region_4.4_spmd} | conditional | flops 282531840 | bytes 16373784 | solution.py:54
  125.4 2.2 %fusion = (f32[16,128]{1,0:T(8,128)S(1)}, f32[16,512,128]{2,1,0:T(8,128)S(1)}) fusion(pred[128,512]{0,1:T(8,128)(4,1)S(1)} %compare_and_fusion, bf16[128,16,64]{0,2,1:T(8,128)(2,1)S(1)} %get-tuple-element.270, bf16[2048,16,64]{0,2,1:T(8,128)(2,1)} %get-tuple-element.268, s32[]{:T(128)} %get-tuple-element.269), kind=kOutput, calls=%fused_computation.2 | convolution fusion | flops 137361408 | bytes 5579264 | tf_op jit(solution)/shard_map/while/body/eval_jaxpr/cond/branch_0_fun/qhd,khd->hqk/dot_general | solution.py:25
  127.6 2.7 %fusion.9 = f32[128,16,64]{0,2,1:T(8,128)S(1)} fusion(f32[16,512,128]{2,1,0:T(8,128)S(1)} %get-tuple-element.329, f32[16,128]{1,0:T(8,128)S(1)} %get-tuple-element.405, pred[128,512]{0,1:T(8,128)(4,1)S(1)} %compare_and_fusion, bf16[2048,16,64]{0,2,1:T(8,128)(2,1)} %get-tuple-element.273, s32[]{:T(128)} %get-tuple-element.269, ...), kind=kOutput, calls=%fused_computation.8 | convolution fusion | flops 139722752 | bytes 6373888 | tf_op jit(solution)/shard_map/while/body/eval_jaxpr/cond/branch_0_fun/hqk,khd->qhd/dot_general | solution.py:35
  131.5 1.3 convolution_convert_fusion.1
  (53 shorter events, 11.6 us)
Async XLA Ops:
  6.5 124.9 %copy-start = (bf16[1024,1280]{1,0:T(8,128)(2,1)S(1)}, bf16[1024,1280]{1,0:T(8,128)(2,1)}, u32[]{:S(2)}) copy-start(bf16[1024,1280]{1,0:T(8,128)(2,1)} %param.15) | copy-start | bytes 7864324
  6.5 7.8 %copy-start.1 = (s32[128]{0:T(128)S(1)}, s32[128]{0:T(128)}, u32[]{:S(2)}) copy-start(s32[128]{0:T(128)} %param.12) | copy-start | bytes 1540
  6.5 65.2 %all-gather.2.cloned.1.call-start = ((), (), s32[]{:S(2)}) async-start(), calls=%async_computation.1 | async-start | bytes 8912896 | tf_op jit(solution)/shard_map/all_gather | solution.py:12
  14.9 75.7 %all-to-all-start = ((s32[16,1,128]{2,1,0:T(1,128)}), s32[16,1,128]{2,1,0:T(1,128)S(1)}, u32[]{:S(2)}, u32[]{:S(2)}) async-start(s32[16,1,128]{2,1,0:T(1,128)} %stack.2), calls=%async_computation | async-start | bytes 16384 | tf_op jit(solution)/shard_map/all_to_all | solution.py:99
Sparse Core Ops, SparseCore 0:
  14.4 57.2 all-gather.1
